TPU v7x, 32 devices: a whole 2x2x4 slice. The times are simulated.
32 devices in a mesh: freq: 8 (over y, x, core), base: 4 (over z).
Axes of the slice: x: 2, y: 2, z: 4, core: 2. Of those that a mesh axis runs over, the one named last changes fastest.
Arguments:
- visibility: float32 [2, 16, 2048], P(None, 'freq', 'base'), may hold values from -6 to 6
- tile_of: int32 [16, 2048, 1], P('freq', 'base'), may hold values from 0 to 3; in each aligned block of 512 rows (0 to 511, 512 to 1023, ..., all dimensions but the last counted through in order) at most 256 rows name the same one
- u_within: int32 [16, 2048], P('freq', 'base'), may hold values from 0 to 255
- v_cell: int32 [16, 2048], P('freq', 'base'), may hold values from 0 to 1016
- kernel_index: int32 [2, 16, 2048], P(None, 'freq', 'base'), may hold values from 0 to 127
- kernel: float32 [128, 8], replicated, may hold values from 0.1 to 1
- live_count: int32 [16, 4], P('freq', 'base'), may hold values from 64 to 512, as said below
- bin_map: int32 [1024, 1024], P('base'), may hold values from 0 to 511, as said below
Outputs:
- power_map: float32 [1024, 1024], P('freq', 'base')
- spectrum: float32 [512], replicated
Inputs may be any that keep to these rules, and one draw needn't show every extreme that they name: `tile_of`: among the visibilities of one channel on one device, at most 256 name the same tile, and in some device's visibilities a tile is named by exactly 256. `live_count`: the first device along base holds 512 used slots in every channel; the used slots of a device are its first ones. `bin_map`: every bin number occurs.
All inputs are finite; a program needn't handle non-finite values.
Results may differ from a plain program's by a relative error of at most 0.0003.
Values sent between devices are 32-bit elements; how exact they have to be, the bound alone decides.
A program may use at most 128 MiB of HBM per device.

v0:
```python
import functools
import math

import jax
import jax.numpy as jnp
import numpy as np
from jax import lax
from jax.experimental import pallas as pl
from jax.experimental.pallas import tpu as pltpu
from jax.sharding import PartitionSpec as P

NBINS = 512
BIN_LOW = 32
KW = 8
FINE = 32
SPREAD = FINE + KW
RADIX = 4
GROUP = 16
FIELDS = 6
LANES = 128
MESH = pl.DeviceIdType.MESH


def halves_of(x):
    high = x.astype(jnp.bfloat16)
    low = (x - high.astype(jnp.float32)).astype(jnp.bfloat16)
    return high, low


@functools.lru_cache(None)
def transform_tables(grid):
    slab = grid // RADIX
    order = np.arange(slab)
    u = 2 * RADIX * (order % (slab // 2)) + RADIX * (order // (slab // 2))
    u = u[None, None, :] + np.arange(RADIX)[:, None, None]
    angle = ((np.arange(slab)[None, :, None] * u) % grid) * (2.0 * math.pi / grid)
    x = np.concatenate([np.cos(angle), np.sin(angle)], axis=1).astype(np.float32)
    high = x.astype(jnp.bfloat16)
    low = (x - high.astype(np.float32)).astype(jnp.bfloat16)
    return high, low


def dot(a, b):
    return jnp.dot(a, b, preferred_element_type=jnp.float32)


def dot_rows(a, b):
    return lax.dot_general(a, b, (((1,), (1,)), ((), ())), preferred_element_type=jnp.float32)


def in_hbm(x):
    return pltpu.with_memory_space_constraint(x, pltpu.HBM)


def greet(peers):
    barrier = pltpu.get_barrier_semaphore()
    for peer in peers:
        pl.semaphore_signal(barrier, inc=1, device_id=peer, device_id_type=MESH)
    return barrier


def phase(product, grid):
    half = grid // 2
    angle = ((product + half) & (grid - 1)) - half
    angle = angle.astype(jnp.float32) * (2.0 * math.pi / grid)
    return jnp.cos(angle), jnp.sin(angle)


def column_tables(grid, split, fine_ref, coarse_ref):
    cols = fine_ref.shape[0] // 2
    coarse_count = grid // FINE
    left = (lax.axis_index("base") * split + lax.rem(lax.axis_index("freq"), split)) * cols
    l = left + lax.broadcasted_iota(jnp.int32, (cols, SPREAD), 0)
    c, s = phase(l * lax.broadcasted_iota(jnp.int32, (cols, SPREAD), 1), grid)
    fine = jnp.concatenate(
        [jnp.concatenate([c, s], axis=1), jnp.concatenate([-s, c], axis=1)], axis=0
    )
    fh, fl = halves_of(fine)
    fine_ref[...] = jnp.zeros_like(fine_ref)
    fine_ref[:, 0:2 * SPREAD] = fh
    fine_ref[:, 2 * SPREAD:4 * SPREAD] = fl
    fine_ref[:, 4 * SPREAD:6 * SPREAD] = fh
    l = lax.broadcasted_iota(jnp.int32, (coarse_count, coarse_count), 0)
    c, s = phase(l * lax.broadcasted_iota(jnp.int32, (coarse_count, coarse_count), 1) * FINE, grid)
    ch, cl = halves_of(jnp.concatenate([c, -s], axis=0))
    coarse_ref[:, 0:coarse_count] = ch
    coarse_ref[:, coarse_count:] = cl


def gather_kernel(
    split, base_count, tile_rows, grid, vis_hbm, tile_hbm, within_hbm, column_hbm, index_hbm, live_hbm,
    taps_hbm, out_ref, fine_ref, coarse_ref, taps_ref,
    vis_ref, tile_ref, within_ref, column_ref, index_ref, live_ref, load_sems, send_sems, recv_sems
):
    freq, base = lax.axis_index("freq"), lax.axis_index("base")
    part = lax.rem(freq, split)
    first = freq - part
    line = [{"freq": freq, "base": lax.rem(base + d, base_count)} for d in range(1, base_count)]
    mates = [{"freq": first + lax.rem(part + d, split), "base": base} for d in range(1, split)]
    barrier = greet(line + mates)
    loads = [
        pltpu.make_async_copy(a, b, load_sems.at[n])
        for n, (a, b) in enumerate([
            (vis_hbm, vis_ref), (tile_hbm, tile_ref), (within_hbm, within_ref), (column_hbm, column_ref),
            (index_hbm, index_ref), (live_hbm, live_ref), (taps_hbm, taps_ref),
        ])
    ]
    for load in loads:
        load.start()
    for load in loads:
        load.wait()
    channels, slots = within_ref.shape
    lane = lax.broadcasted_iota(jnp.int32, (1, slots), 1)
    for c in range(channels):
        is_live = lane < live_ref[0:1, c:c + 1]
        u = jnp.minimum(tile_ref[c] * tile_rows + within_ref[c:c + 1, :], grid - KW)
        fields = [
            jnp.where(is_live, vis_ref[0, c:c + 1, :], 0.0),
            jnp.where(is_live, vis_ref[1, c:c + 1, :], 0.0),
            u.astype(jnp.float32),
            column_ref[c:c + 1, :].astype(jnp.float32),
            jnp.where(is_live, index_ref[0, c:c + 1, :], -1).astype(jnp.float32),
            index_ref[1, c:c + 1, :].astype(jnp.float32),
        ]
        rows = [x[:, at:at + LANES] for x in fields for at in range(0, slots, LANES)]
        out_ref[part * channels + c, base] = jnp.concatenate(rows, axis=0)
    column_tables(grid, split, fine_ref, coarse_ref)
    pl.semaphore_wait(barrier, len(line) + len(mates))

    def block_copy(owner, peer, k):
        block = out_ref.at[pl.ds(part * channels, channels), owner]
        return pltpu.make_async_remote_copy(
            src_ref=block, dst_ref=block, send_sem=send_sems.at[k], recv_sem=recv_sems.at[k],
            device_id=peer, device_id_type=MESH,
        )

    sent = [block_copy(base, peer, k) for k, peer in enumerate(line)]
    for copy in sent:
        copy.start()
    passed = []
    for d in range(base_count):
        if d:
            sent[d - 1].wait_recv()
        for k, mate in enumerate(mates):
            copy = block_copy(
                lax.rem(base + base_count - d, base_count), mate, len(line) + k * base_count + d
            )
            copy.start()
            passed.append(copy)
    for copy in passed:
        copy.wait()
    for copy in sent:
        copy.wait_send()


def gather_fields(split, base_count, tile_rows, grid, cols, *arrays):
    channels, slots = arrays[2].shape
    sems = base_count - 1 + (split - 1) * base_count
    total = channels * split
    f32, bf16 = jnp.float32, jnp.bfloat16
    vmem = pl.BlockSpec(memory_space=pltpu.VMEM)
    hbm = pl.BlockSpec(memory_space=pltpu.HBM)
    return pl.pallas_call(
        functools.partial(gather_kernel, split, base_count, tile_rows, grid),
        out_shape=(
            jax.ShapeDtypeStruct((total, base_count, FIELDS * (slots // LANES), LANES), f32),
            jax.ShapeDtypeStruct((2 * cols, 256), bf16),
            jax.ShapeDtypeStruct((2 * (grid // FINE), 2 * (grid // FINE)), bf16),
            jax.ShapeDtypeStruct(arrays[-1].shape, f32),
        ),
        in_specs=[hbm] * len(arrays),
        out_specs=(vmem,) * 4,
        scratch_shapes=[pltpu.VMEM(x.shape, x.dtype) for x in arrays[:-1]] + [
            pltpu.SemaphoreType.DMA((len(arrays),)),
            pltpu.SemaphoreType.DMA((sems,)), pltpu.SemaphoreType.DMA((sems,)),
        ],
        compiler_params=pltpu.CompilerParams(
            collective_id=0, has_side_effects=True, vmem_limit_bytes=12 * 2**20
        ),
        name="gather_fields",
    )(*[in_hbm(x) for x in arrays])


def grid_kernel(
    grid, f_ref, fine_ref, coarse_ref, kernel_ref, h_ref,
    spread_ref, pick_ref, z_ref, tap_ref, spot_ref, channel_ref
):
    channels, blocks, rows, _ = f_ref.shape
    subs = rows // FIELDS
    cols = h_ref.shape[3] // 2
    half = grid // (2 * RADIX)
    coarse_count = grid // FINE
    piece = 2 * LANES
    tap_table = kernel_ref[...]
    h_ref[...] = jnp.zeros_like(h_ref)

    counts = []
    for c in range(channels):
        for b in range(blocks):
            used = f_ref[c, b, 4 * subs:5 * subs, :] >= 0.0
            counts.append(jnp.sum(jnp.where(used, 1.0, 0.0)))
    filled = jnp.int32(0)
    for c in range(channels):
        for b in range(blocks):
            for sub in range(subs):
                spot_ref[filled + sub] = b * subs + sub
            for ahead in range(subs // 2 + 1):
                channel_ref[lax.shift_right_logical(filled, jnp.int32(1)) + ahead] = c
            count = counts[c * blocks + b].astype(jnp.int32)
            filled = filled + lax.shift_right_logical(count + (LANES - 1), jnp.int32(LANES.bit_length() - 1))
        spot_ref[filled] = -1
        filled = (filled + 1) & -2
    steps = lax.shift_right_logical(filled, jnp.int32(1))
    for ahead in range(8):
        spot_ref[filled + ahead] = -1
    for ahead in range(4):
        channel_ref[steps + ahead] = 0

    def field(step, number):
        c = channel_ref[step]
        one, two = jnp.maximum(spot_ref[2 * step], 0), jnp.maximum(spot_ref[2 * step + 1], 0)
        by = jnp.int32(subs.bit_length() - 1)
        return jnp.concatenate(
            [
                f_ref[c, lax.shift_right_logical(one, by), pl.ds(number * subs + (one & (subs - 1)), 1), :],
                f_ref[c, lax.shift_right_logical(two, by), pl.ds(number * subs + (two & (subs - 1)), 1), :],
            ],
            axis=1,
        )

    def look_up(table, row):
        row = jnp.maximum(row.astype(jnp.int32), 0)
        pieces = []
        for at in range(0, piece, LANES):
            index = jnp.broadcast_to(row[:, at:at + LANES], (KW, LANES))
            pieces.append(jnp.take_along_axis(table, index, axis=1))
        return jnp.concatenate(pieces, axis=1)

    lane = lax.broadcasted_iota(jnp.int32, (1, piece), 1)

    def make_spread(step, slot):
        keep = lane < jnp.where(
            spot_ref[2 * step + 1] >= 0, piece, jnp.where(spot_ref[2 * step] >= 0, LANES, 0)
        )
        re = jnp.where(keep, field(step, 0), 0.0)
        im = jnp.where(keep, field(step, 1), 0.0)
        v = field(step, 3).astype(jnp.int32)
        taps_v = look_up(tap_table, field(step, 5))
        offset = lax.broadcasted_iota(jnp.int32, (SPREAD, piece), 0) - (v & (FINE - 1))
        spread = jnp.zeros((SPREAD, piece), jnp.float32)
        for t in range(KW):
            spread = jnp.where(offset == t, taps_v[t:t + 1, :], spread)
        both = jnp.concatenate([spread * re, spread * im], axis=0)
        bh, bl = halves_of(both)
        pad = jnp.zeros((256 - 6 * SPREAD, piece), jnp.bfloat16)
        spread_ref[slot] = jnp.concatenate([bh, bh, bl, pad], axis=0)
        pick = lax.broadcasted_iota(jnp.int32, (2 * coarse_count, piece), 0) & (coarse_count - 1)
        pick_ref[slot] = jnp.where(pick == v // FINE, 1.0, 0.0).astype(jnp.bfloat16)

    def make_z(step, slot):
        zb = dot(fine_ref[...], spread_ref[slot])
        e = dot(coarse_ref[...], pick_ref[slot])
        er, ei = e[:coarse_count], e[coarse_count:]
        re, im = [], []
        for at in range(0, cols, coarse_count):
            zr, zi = zb[at:at + coarse_count], zb[cols + at:cols + at + coarse_count]
            re.append(zr * er - zi * ei)
            im.append(zr * ei + zi * er)
        for n, parts in enumerate((re, im)):
            zh, zl = halves_of(jnp.concatenate(parts, axis=0).T)
            z_ref[slot, 0, :, n * cols:(n + 1) * cols] = zh
            z_ref[slot, 1, :, n * cols:(n + 1) * cols] = zl

        u = field(step, 2).astype(jnp.int32)
        taps_u = look_up(tap_table, field(step, 4))
        residue = lax.broadcasted_iota(jnp.int32, (2 * RADIX, piece), 0)
        tap = (residue - u) & (2 * RADIX - 1)
        row = lax.shift_right_logical(u + tap, jnp.int32((2 * RADIX).bit_length() - 1))
        weight = jnp.zeros((2 * RADIX, piece), jnp.float32)
        for t in range(KW):
            weight = jnp.where(tap == t, taps_u[t:t + 1, :], weight)
        high = weight.astype(jnp.bfloat16).astype(jnp.float32)
        tap_ref[slot, 0] = row.astype(jnp.float32)
        tap_ref[slot, 1] = high
        tap_ref[slot, 2] = weight - high

    def add_rows(step, slot):
        c = channel_ref[step]
        rows16 = lax.broadcasted_iota(jnp.int32, (GROUP, piece), 0).astype(jnp.float32)
        spots = [(rows16 + float(at)).astype(jnp.bfloat16) for at in range(0, half, GROUP)]

        def wide(kind, residue):
            x = tap_ref[slot, kind, residue:residue + 1, :]
            return jnp.broadcast_to(x, (GROUP, piece)).astype(jnp.bfloat16)

        for first in range(RADIX):
            highs, lows = [], []
            for residue in (first, first + RADIX):
                row, high, low = (wide(kind, residue) for kind in range(3))
                zero = jnp.zeros_like(high)
                for spot in spots:
                    hit = row == spot
                    highs.append(jnp.where(hit, high, zero))
                    lows.append(jnp.where(hit, low, zero))
            wh, wl = jnp.concatenate(highs, axis=0), jnp.concatenate(lows, axis=0)
            zh, zl = z_ref[slot, 0], z_ref[slot, 1]
            h_ref[c, first] += dot(wh, zh) + dot(wh, zl) + dot(wl, zh)

    make_spread(0, 0)
    make_z(0, 0)
    make_spread(1, 1)

    def two_steps(n, carry):
        for slot in range(2):
            step = 2 * n + slot
            make_z(step + 1, 1 - slot)
            add_rows(step, slot)
            make_spread(step + 2, slot)
        return carry

    lax.fori_loop(0, (steps + 1) // 2, two_steps, 0)


def grid_visibilities(fields, fine, coarse, taps_table, grid):
    both = fine.shape[0]
    channels, blocks, rows, _ = fields.shape
    most = channels * (blocks * (rows // FIELDS) + 1)
    smem = lambda n: pltpu.SMEM((n,), jnp.int32)
    vmem = pl.BlockSpec(memory_space=pltpu.VMEM)
    return pl.pallas_call(
        functools.partial(grid_kernel, grid),
        out_shape=jax.ShapeDtypeStruct((channels, RADIX, grid // RADIX, both), jnp.float32),
        in_specs=[vmem] * 4,
        out_specs=vmem,
        scratch_shapes=[
            pltpu.VMEM((2, 256, 2 * LANES), jnp.bfloat16),
            pltpu.VMEM((2, 2 * (grid // FINE), 2 * LANES), jnp.bfloat16),
            pltpu.VMEM((2, 2, 2 * LANES, both), jnp.bfloat16),
            pltpu.VMEM((2, 3, 2 * RADIX, 2 * LANES), jnp.float32),
            smem(most + 16), smem(most // 2 + 16),
        ],
        compiler_params=pltpu.CompilerParams(vmem_limit_bytes=16 * 2**20),
        name="grid_visibilities",
    )(fields, fine, coarse, taps_table)


def power_kernel(
    grid, freq_count, base_count, split, scale, h_ref, dh_hbm, dl_hbm, bins_hbm, share_ref, spectrum_ref,
    dh_ref, dl_ref, bins_ref, load_sems, bins_sem, hh_ref, hl_ref, y_ref, power_ref, recv_ref, mask_ref, value_ref, low_ref, stage_ref, stage2_ref,
    send_sems, recv_sems, sum_send_sems, sum_recv_sems
):
    freq, base = lax.axis_index("freq"), lax.axis_index("base")
    ring = [{"freq": lax.rem(freq + d, freq_count), "base": base} for d in range(1, freq_count)]
    line = [{"freq": freq, "base": lax.rem(base + d, base_count)} for d in range(1, base_count)]
    barrier = greet(ring + line)
    loads = []
    for n in range(RADIX):
        loads.append(pltpu.make_async_copy(dh_hbm.at[n], dh_ref.at[n], load_sems.at[0, n]))
        loads.append(pltpu.make_async_copy(dl_hbm.at[n], dl_ref.at[n], load_sems.at[1, n]))
    for load in loads:
        load.start()
    rows_here = bins_ref.shape[1]
    if bins_hbm.shape[1] != rows_here:
        here = pl.ds(pl.multiple_of(freq * rows_here, rows_here), rows_here)
        load_bins = pltpu.make_async_copy(bins_hbm.at[:, here], bins_ref, bins_sem)
    else:
        load_bins = pltpu.make_async_copy(bins_hbm, bins_ref, bins_sem)
    load_bins.start()

    channels = h_ref.shape[0]
    slab = grid // RADIX
    share_rows, width = share_ref.shape
    cols = width // split
    chunk = min(64, share_rows)
    parts = share_rows // chunk
    shares = slab // share_rows

    def split_rows(n, carry):
        high, low = halves_of(h_ref[n // RADIX, n % RADIX])
        hh_ref[n // RADIX, n % RADIX] = high
        hl_ref[n // RADIX, n % RADIX] = low
        return carry

    lax.fori_loop(0, channels * RADIX, split_rows, 0)
    for load in loads:
        load.wait()

    def transform(n):
        top = pl.multiple_of((lax.rem(n, shares) * parts + n // shares) * chunk, chunk)
        for c in range(channels):
            for first in range(RADIX):
                dh = jnp.concatenate(
                    [dh_ref[first, pl.ds(top, chunk), :], dh_ref[first, pl.ds(slab + top, chunk), :]], axis=0
                )
                dl = jnp.concatenate(
                    [dl_ref[first, pl.ds(top, chunk), :], dl_ref[first, pl.ds(slab + top, chunk), :]], axis=0
                )
                hh, hl = hh_ref[c, first], hl_ref[c, first]
                y_ref[c % 2, first] = dot(dh, hh) + dot(dl, hh) + dot(dh, hl)
            step = min(16, chunk)
            for row in range(0, chunk, step):
                yr, yi = [], []
                for first in range(RADIX):
                    cy = y_ref[c % 2, first, row:row + step, :]
                    sy = y_ref[c % 2, first, chunk + row:chunk + row + step, :]
                    yr.append(cy[:, :cols] + sy[:, cols:])
                    yi.append(cy[:, cols:] - sy[:, :cols])
                ar, ai = yr[0] + yr[2], yi[0] + yi[2]
                br, bi = yr[0] - yr[2], yi[0] - yi[2]
                cr, ci = yr[1] + yr[3], yi[1] + yi[3]
                dr, di = yr[1] - yr[3], yi[1] - yi[3]
                outs = [
                    (ar + cr, ai + ci), (br + di, bi - dr), (ar - cr, ai - ci), (br - di, bi + dr)
                ]
                for k, (xr, xi) in enumerate(outs):
                    at = pl.ds(pl.multiple_of(k * slab + top + row, step), step)
                    value = (xr * xr + xi * xi) * scale
                    power_ref[at, :] = value if c == 0 else power_ref[at, :] + value

    def piece(n, k):
        share, part = lax.rem(n, shares), n // shares
        target = k * shares + share
        top = pl.multiple_of(target * share_rows + part * chunk, chunk)
        rows = pl.ds(pl.multiple_of(part * chunk, chunk), chunk)
        copy = pltpu.make_async_remote_copy(
            src_ref=power_ref.at[pl.ds(top, chunk), :],
            dst_ref=recv_ref.at[freq, rows, :],
            send_sem=send_sems.at[n, k], recv_sem=recv_sems.at[freq, part],
            device_id={"freq": target, "base": base}, device_id_type=MESH,
        )
        return target, top, rows, copy

    def send(n):
        for k in range(RADIX):
            target, top, rows, copy = piece(n, k)

            @pl.when(target == freq)
            def _():
                recv_ref[freq, rows, :] = power_ref[pl.ds(top, chunk), :]

            @pl.when(target != freq)
            def _():
                copy.start()

    transform(0)
    pl.semaphore_wait(barrier, len(ring) + len(line))
    send(0)

    def later(n, carry):
        transform(n)
        send(n)
        return carry

    lax.fori_loop(1, shares * parts, later, 0)

    high_count = NBINS // BIN_LOW
    lead = high_count // 4
    load_bins.wait()
    bins = bins_ref[...].T
    order = lax.broadcasted_iota(jnp.int32, (high_count, width), 0)
    order = lead * (order % lead) + order // lead if lead == 4 else order
    low_order = lax.broadcasted_iota(jnp.int32, (BIN_LOW, width), 0)
    for row in range(share_rows):
        at = slice(row * width, (row + 1) * width)
        bin_id = bins[row:row + 1, :]
        mask_ref[:, at] = jnp.where(order == bin_id // BIN_LOW, 1.0, 0.0).astype(jnp.bfloat16)
        low_ref[:, at] = jnp.where(low_order == bin_id % BIN_LOW, 1.0, 0.0).astype(jnp.bfloat16)
    counts = dot_rows(mask_ref[...], low_ref[...])

    totals = jnp.zeros((high_count, BIN_LOW), jnp.float32)
    for part in range(parts):
        rows = slice(part * chunk, (part + 1) * chunk)
        for d in range(1, freq_count):
            source = lax.rem(freq + d, freq_count)
            pltpu.make_async_remote_copy(
                src_ref=power_ref.at[0:chunk, :], dst_ref=recv_ref.at[source, rows, :],
                send_sem=send_sems.at[0, 0], recv_sem=recv_sems.at[source, part],
                device_id={"freq": source, "base": base}, device_id_type=MESH,
            ).wait_recv()
        for half in range(split):
            total = recv_ref[half, rows, :]
            for group in range(1, freq_count // split):
                total = total + recv_ref[group * split + half, rows, :]
            share_ref[rows, half * cols:(half + 1) * cols] = total
        for row in range(part * chunk, (part + 1) * chunk):
            at = slice(row * width, (row + 1) * width)
            out = slice((row - part * chunk) * width, (row - part * chunk + 1) * width)
            value = jnp.broadcast_to(share_ref[row:row + 1, :], (high_count, width))
            high, low = halves_of(value)
            mask = mask_ref[:, at]
            value_ref[0:high_count, out] = mask * high
            value_ref[high_count:, out] = mask * low
        span = slice(part * chunk * width, (part + 1) * chunk * width)
        sums = dot_rows(value_ref[...], low_ref[:, span])
        totals = totals + sums[:high_count] + sums[high_count:]

    def pack(x):
        return jnp.concatenate([x[lead * k:lead * (k + 1)] for k in range(4)], axis=1)

    stage_ref[freq] = jnp.concatenate([pack(totals), pack(counts)], axis=0)

    def share_out(ref, me, peers, offset):
        copies = []
        for k, peer in enumerate(peers):
            copy = pltpu.make_async_remote_copy(
                src_ref=ref.at[me], dst_ref=ref.at[me],
                send_sem=sum_send_sems.at[offset + k], recv_sem=sum_recv_sems.at[offset + k],
                device_id=peer, device_id_type=MESH,
            )
            copy.start()
            copies.append(copy)
        for copy in copies:
            copy.wait()
        total = ref[0]
        for other in range(1, ref.shape[0]):
            total = total + ref[other]
        return total

    stage2_ref[base] = share_out(stage_ref, freq, ring, 0)
    total = share_out(stage2_ref, base, line, len(ring))
    spectrum_ref[...] = total[:lead] / total[lead:]

    def finish(n, carry):
        for k in range(RADIX):
            target, _, _, copy = piece(n, k)

            @pl.when(target != freq)
            def _():
                copy.wait_send()
        return carry

    lax.fori_loop(0, shares * parts, finish, 0)


def power_and_spectrum(h, dh, dl, bins, grid, freq_count, base_count, split, width, scale):
    channels, _, slab, both = h.shape
    cols = both // 2
    share_rows = grid // freq_count
    chunk = min(64, share_rows)
    parts, shares = share_rows // chunk, slab // share_rows
    high_count = NBINS // BIN_LOW
    cells = share_rows * width
    sems = freq_count + base_count - 2
    f32, bf16 = jnp.float32, jnp.bfloat16
    vmem = pl.BlockSpec(memory_space=pltpu.VMEM)
    hbm = pl.BlockSpec(memory_space=pltpu.HBM)
    return pl.pallas_call(
        functools.partial(power_kernel, grid, freq_count, base_count, split, scale),
        out_shape=(
            jax.ShapeDtypeStruct((share_rows, width), f32),
            jax.ShapeDtypeStruct((4, 4 * BIN_LOW), f32),
        ),
        in_specs=[vmem, hbm, hbm, hbm],
        out_specs=(vmem, vmem),
        scratch_shapes=[
            pltpu.VMEM(dh.shape, bf16),
            pltpu.VMEM(dl.shape, bf16),
            pltpu.VMEM((bins.shape[0], share_rows), jnp.int32),
            pltpu.SemaphoreType.DMA((2, RADIX)),
            pltpu.SemaphoreType.DMA,
            pltpu.VMEM(h.shape, bf16),
            pltpu.VMEM(h.shape, bf16),
            pltpu.VMEM((2, RADIX, 2 * chunk, both), f32),
            pltpu.VMEM((grid, cols), f32),
            pltpu.VMEM((freq_count, share_rows, cols), f32),
            pltpu.VMEM((high_count, cells), bf16),
            pltpu.VMEM((2 * high_count, chunk * width), bf16),
            pltpu.VMEM((BIN_LOW, cells), bf16),
            pltpu.VMEM((freq_count, 8, 4 * BIN_LOW), f32),
            pltpu.VMEM((base_count, 8, 4 * BIN_LOW), f32),
            pltpu.SemaphoreType.DMA((shares * parts, RADIX)),
            pltpu.SemaphoreType.DMA((freq_count, parts)),
            pltpu.SemaphoreType.DMA((sems,)),
            pltpu.SemaphoreType.DMA((sems,)),
        ],
        compiler_params=pltpu.CompilerParams(
            collective_id=1, has_side_effects=True, vmem_limit_bytes=24 * 2**20
        ),
        name="power_and_spectrum",
    )(h, in_hbm(dh), in_hbm(dl), in_hbm(bins))


def per_device(visibility, tile_of, u_within, v_cell, kernel_index, kernel, live_count, bin_map):
    base_count = lax.axis_size("base")
    freq_count = lax.axis_size("freq")
    grid = bin_map.shape[1]
    width = grid // base_count
    split = 2 if width % (2 * LANES) == 0 and freq_count % 2 == 0 else 1
    channels_here, slots = u_within.shape
    dh, dl = transform_tables(grid)
    scale = 1.0 / (channels_here * freq_count * slots * base_count)
    gathered = gather_fields(
        split, base_count, grid // base_count, grid, width // split,
        visibility, tile_of.transpose(0, 2, 1), u_within, v_cell, kernel_index, live_count.T, kernel.T,
    )
    h = grid_visibilities(*gathered, grid)
    share_rows = grid // freq_count
    bins = bin_map
    if share_rows % LANES:
        bins = lax.dynamic_slice_in_dim(bin_map, lax.axis_index("freq") * share_rows, share_rows, 1)
    share, spectrum = power_and_spectrum(
        h, jnp.asarray(dh), jnp.asarray(dl), bins, grid, freq_count, base_count, split, width, scale
    )
    return share, spectrum.reshape(NBINS)


def solution(mesh):
    in_specs = (
        P(None, "freq", "base"),
        P("freq", "base", None),
        P("freq", "base"),
        P("freq", "base"),
        P(None, "freq", "base"),
        P(),
        P("freq", "base"),
        P("base", None),
    )
    out_specs = (P("freq", "base"), P())
    return jax.shard_map(
        per_device, mesh=mesh, in_specs=in_specs, out_specs=out_specs, check_vma=False
    )
```

profile of v0, /device:TPU:0, one launch (start us, length us, event | category | flops | bytes accessed | tf_op | source)
XLA Modules:
  0.0 43.5 jit_solution(14878924392402865839)
XLA Ops:
  0.6 9.3 %gather_fields.1 = (f32[4,4,24,128]{3,2,1,0:T(8,128)S(1)}, bf16[256,256]{1,0:T(8,128)(2,1)S(1)}, bf16[64,64]{1,0:T(8,128)(2,1)S(1)}, f32[8,128]{1,0:T(8,128)S(1)}) custom-call(f32[2,2,512]{2,1,0:T(2,128)} %vis_hbm.1, s32[2,1,512]{2,1,0:T(1,128)} %bitcast.5, s32[2,512]{1,0:T(2,128)} %within_hbm.1, s32[2,512]{1,0:T(2,128)} %column_hbm.1, ...), custom_call_target="tpu_custom_call" | custom-call | tf_op jit(solution)/shard_map/gather_fields/pallas_call | solution.py:163
  10.0 12.9 %grid_visibilities.1.h_ref = f32[4,4,256,256]{3,2,1,0:T(8,128)S(1)} custom-call(f32[4,4,24,128]{3,2,1,0:T(8,128)S(1)} %get-tuple-element.8.f_ref, bf16[256,256]{1,0:T(8,128)(2,1)S(1)} %get-tuple-element.9.fine_ref, bf16[64,64]{1,0:T(8,128)(2,1)S(1)} %get-tuple-element.10.coarse_ref, f32[8,128]{1,0:T(8,128)S(1)} %get-tuple-element.11.kernel_ref), custom_call_target="tpu_custom_call" | custom-call | tf_op jit(solution)/shard_map/grid_visibilities/pallas_call | solution.py:330
  22.9 19.4 %power_and_spectrum.1 = (f32[128,256]{1,0:T(8,128)S(1)}, f32[4,128]{1,0:T(4,128)S(1)}) custom-call(f32[4,4,256,256]{3,2,1,0:T(8,128)S(1)} %grid_visibilities.1.h_ref, bf16[4,512,256]{2,1,0:T(8,128)(2,1)} %constant.4.clone.dh_hbm, bf16[4,512,256]{2,1,0:T(8,128)(2,1)} %constant.5.clone.dl_hbm, s32[256,1024]{1,0:T(8,128)} %bins_hbm.1), custom_call_target="tpu_custom_call" | custom-call | tf_op jit(solution)/shard_map/power_and_spectrum/pallas_call | solution.py:547
  42.3 0.7 %copy.14 = f32[128,256]{1,0:T(8,128)} copy(f32[128,256]{1,0:T(8,128)S(1)} %get-tuple-element.16) | data formatting | bytes 262144
  43.0 0.6 %copy.15 = f32[512]{0:T(512)} copy(f32[512]{0:T(512)S(1)} %bitcast.4) | data formatting | bytes 4096
where the time goes:
time: 43.8 us; the launch traced here: 43.5 us
  Pallas kernels  41.7 us (95%)
  local copies, waits for them, and re-layouts  1.24 us (3%)
  between operations  0.66 us (2%)
    pallas_call x1, Pallas kernels, power_and_spectrum(): pl.pallas_call(functools.partial(power_kernel, grid, freq_count, base_cou...  19.4 us
    pallas_call x1, Pallas kernels, grid_visibilities(): pl.pallas_call(functools.partial(grid_kernel, grid), out_shape=jax.ShapeD...  12.9 us
    pallas_call x1, Pallas kernels, gather_fields(): pl.pallas_call(functools.partial(gather_kernel, split, base_count, tile_r...  9.34 us
    unnamed x2, local copies, waits for them, and re-layouts  1.24 us

commit v1 on v0

--- a/solution.py
+++ b/solution.py
@@ -87,10 +87,104 @@
     coarse_ref[:, coarse_count:] = cl
 
 
+def look_up(table, row):
+    row = jnp.maximum(row.astype(jnp.int32), 0)
+    pieces = []
+    for at in range(0, row.shape[1], LANES):
+        index = jnp.broadcast_to(row[:, at:at + LANES], (KW, LANES))
+        pieces.append(jnp.take_along_axis(table, index, axis=1))
+    return jnp.concatenate(pieces, axis=1)
+
+
+def store_spread(grid, table, field, keep, slot, spread_ref, pick_ref):
+    re, im = field(0), field(1)
+    if keep is not None:
+        re, im = jnp.where(keep, re, 0.0), jnp.where(keep, im, 0.0)
+    piece = re.shape[1]
+    coarse_count = grid // FINE
+    v = field(3).astype(jnp.int32)
+    taps_v = look_up(table, field(5))
+    offset = lax.broadcasted_iota(jnp.int32, (SPREAD, piece), 0) - (v & (FINE - 1))
+    spread = jnp.zeros((SPREAD, piece), jnp.float32)
+    for t in range(KW):
+        spread = jnp.where(offset == t, taps_v[t:t + 1, :], spread)
+    both = jnp.concatenate([spread * re, spread * im], axis=0)
+    bh, bl = halves_of(both)
+    pad = jnp.zeros((256 - 6 * SPREAD, piece), jnp.bfloat16)
+    spread_ref[slot] = jnp.concatenate([bh, bh, bl, pad], axis=0)
+    pick = lax.broadcasted_iota(jnp.int32, (2 * coarse_count, piece), 0) & (coarse_count - 1)
+    pick_ref[slot] = jnp.where(pick == v // FINE, 1.0, 0.0).astype(jnp.bfloat16)
+
+
+def store_z(grid, table, field, slot, fine_ref, coarse_ref, spread_ref, pick_ref, z_ref, tap_ref):
+    cols = fine_ref.shape[0] // 2
+    coarse_count = grid // FINE
+    zb = dot(fine_ref[...], spread_ref[slot])
+    e = dot(coarse_ref[...], pick_ref[slot])
+    er, ei = e[:coarse_count], e[coarse_count:]
+    re, im = [], []
+    for at in range(0, cols, coarse_count):
+        zr, zi = zb[at:at + coarse_count], zb[cols + at:cols + at + coarse_count]
+        re.append(zr * er - zi * ei)
+        im.append(zr * ei + zi * er)
+    for n, parts in enumerate((re, im)):
+        zh, zl = halves_of(jnp.concatenate(parts, axis=0).T)
+        z_ref[slot, 0, :, n * cols:(n + 1) * cols] = zh
+        z_ref[slot, 1, :, n * cols:(n + 1) * cols] = zl
+
+    u = field(2).astype(jnp.int32)
+    taps_u = look_up(table, field(4))
+    residue = lax.broadcasted_iota(jnp.int32, (2 * RADIX, u.shape[1]), 0)
+    tap = (residue - u) & (2 * RADIX - 1)
+    row = lax.shift_right_logical(u + tap, jnp.int32((2 * RADIX).bit_length() - 1))
+    weight = jnp.zeros(tap.shape, jnp.float32)
+    for t in range(KW):
+        weight = jnp.where(tap == t, taps_u[t:t + 1, :], weight)
+    high = weight.astype(jnp.bfloat16).astype(jnp.float32)
+    tap_ref[slot, 0] = row.astype(jnp.float32)
+    tap_ref[slot, 1] = high
+    tap_ref[slot, 2] = weight - high
+
+
+def slab_of(grid, first, slot, z_ref, tap_ref):
+    half = grid // (2 * RADIX)
+    piece = tap_ref.shape[3]
+    rows16 = lax.broadcasted_iota(jnp.int32, (GROUP, piece), 0).astype(jnp.float32)
+    spots = [(rows16 + float(at)).astype(jnp.bfloat16) for at in range(0, half, GROUP)]
+
+    def wide(kind, residue):
+        x = tap_ref[slot, kind, residue:residue + 1, :]
+        return jnp.broadcast_to(x, (GROUP, piece)).astype(jnp.bfloat16)
+
+    highs, lows = [], []
+    for residue in (first, first + RADIX):
+        row, high, low = (wide(kind, residue) for kind in range(3))
+        zero = jnp.zeros_like(high)
+        for spot in spots:
+            hit = row == spot
+            highs.append(jnp.where(hit, high, zero))
+            lows.append(jnp.where(hit, low, zero))
+    wh, wl = jnp.concatenate(highs, axis=0), jnp.concatenate(lows, axis=0)
+    zh, zl = z_ref[slot, 0], z_ref[slot, 1]
+    return dot(wh, zh) + dot(wh, zl) + dot(wl, zh)
+
+
+def step_scratch(grid, both):
+    bf16, f32 = jnp.bfloat16, jnp.float32
+    piece = 2 * LANES
+    return [
+        pltpu.VMEM((2, 256, piece), bf16),
+        pltpu.VMEM((2, 2 * (grid // FINE), piece), bf16),
+        pltpu.VMEM((2, 2, piece, both), bf16),
+        pltpu.VMEM((2, 3, 2 * RADIX, piece), f32),
+    ]
+
+
 def gather_kernel(
     split, base_count, tile_rows, grid, vis_hbm, tile_hbm, within_hbm, column_hbm, index_hbm, live_hbm,
-    taps_hbm, out_ref, fine_ref, coarse_ref, taps_ref,
-    vis_ref, tile_ref, within_ref, column_ref, index_ref, live_ref, load_sems, send_sems, recv_sems
+    taps_hbm, out_ref, fine_ref, coarse_ref, taps_ref, h_ref,
+    vis_ref, tile_ref, within_ref, column_ref, index_ref, live_ref, load_sems, send_sems, recv_sems,
+    spread_ref, pick_ref, z_ref, tap_ref
 ):
     freq, base = lax.axis_index("freq"), lax.axis_index("base")
     part = lax.rem(freq, split)
@@ -137,18 +231,42 @@
     sent = [block_copy(base, peer, k) for k, peer in enumerate(line)]
     for copy in sent:
         copy.start()
-    passed = []
-    for d in range(base_count):
+    passed = [[] for _ in mates]
+
+    def pass_on(d):
+        owner = lax.rem(base + base_count - d, base_count)
+        for k, mate in enumerate(mates):
+            copy = block_copy(owner, mate, len(line) + k * base_count + d)
+            copy.start()
+            passed[k].append(copy)
+
+    pass_on(0)
+    subs = slots // LANES
+    table = taps_ref[...]
+    for d in range(split):
         if d:
-            sent[d - 1].wait_recv()
-        for k, mate in enumerate(mates):
-            copy = block_copy(
-                lax.rem(base + base_count - d, base_count), mate, len(line) + k * base_count + d
-            )
-            copy.start()
-            passed.append(copy)
-    for copy in passed:
-        copy.wait()
+            passed[split - 1 - d][0].wait_recv()
+        group = lax.rem(part + d, split) * channels
+
+        def field_of(c):
+            def field(number):
+                rows = [out_ref[group + c, base, pl.ds(number * subs + n, 1), :] for n in range(2)]
+                return jnp.concatenate(rows, axis=1)
+            return field
+
+        for c in range(channels):
+            store_spread(grid, table, field_of(c), None, c % 2, spread_ref, pick_ref)
+            store_z(grid, table, field_of(c), c % 2, fine_ref, coarse_ref, spread_ref, pick_ref, z_ref, tap_ref)
+            for residue in range(RADIX):
+                h_ref[group + c, residue] = slab_of(grid, residue, c % 2, z_ref, tap_ref)
+    for d in range(1, base_count):
+        sent[d - 1].wait_recv()
+        pass_on(d)
+    for k in range(len(mates)):
+        for d, copy in enumerate(passed[k]):
+            copy.wait_send()
+            if d:
+                copy.wait_recv()
     for copy in sent:
         copy.wait_send()
 
@@ -167,13 +285,14 @@
             jax.ShapeDtypeStruct((2 * cols, 256), bf16),
             jax.ShapeDtypeStruct((2 * (grid // FINE), 2 * (grid // FINE)), bf16),
             jax.ShapeDtypeStruct(arrays[-1].shape, f32),
+            jax.ShapeDtypeStruct((total, RADIX, grid // RADIX, 2 * cols), f32),
         ),
         in_specs=[hbm] * len(arrays),
-        out_specs=(vmem,) * 4,
+        out_specs=(vmem,) * 5,
         scratch_shapes=[pltpu.VMEM(x.shape, x.dtype) for x in arrays[:-1]] + [
             pltpu.SemaphoreType.DMA((len(arrays),)),
             pltpu.SemaphoreType.DMA((sems,)), pltpu.SemaphoreType.DMA((sems,)),
-        ],
+        ] + step_scratch(grid, 2 * cols),
         compiler_params=pltpu.CompilerParams(
             collective_id=0, has_side_effects=True, vmem_limit_bytes=12 * 2**20
         ),
@@ -182,17 +301,14 @@
 
 
 def grid_kernel(
-    grid, f_ref, fine_ref, coarse_ref, kernel_ref, h_ref,
+    grid, f_ref, fine_ref, coarse_ref, kernel_ref, start_ref, h_ref,
     spread_ref, pick_ref, z_ref, tap_ref, spot_ref, channel_ref
 ):
     channels, blocks, rows, _ = f_ref.shape
     subs = rows // FIELDS
-    cols = h_ref.shape[3] // 2
-    half = grid // (2 * RADIX)
-    coarse_count = grid // FINE
     piece = 2 * LANES
     tap_table = kernel_ref[...]
-    h_ref[...] = jnp.zeros_like(h_ref)
+    base = lax.axis_index("base")
 
     counts = []
     for c in range(channels):
@@ -202,12 +318,14 @@
     filled = jnp.int32(0)
     for c in range(channels):
         for b in range(blocks):
+            done = jnp.where(base == b, 2, 0)
             for sub in range(subs):
-                spot_ref[filled + sub] = b * subs + sub
+                spot_ref[filled + sub] = b * subs + sub + done
             for ahead in range(subs // 2 + 1):
                 channel_ref[lax.shift_right_logical(filled, jnp.int32(1)) + ahead] = c
             count = counts[c * blocks + b].astype(jnp.int32)
-            filled = filled + lax.shift_right_logical(count + (LANES - 1), jnp.int32(LANES.bit_length() - 1))
+            live = lax.shift_right_logical(count + (LANES - 1), jnp.int32(LANES.bit_length() - 1))
+            filled = filled + jnp.maximum(live - done, 0)
         spot_ref[filled] = -1
         filled = (filled + 1) & -2
     steps = lax.shift_right_logical(filled, jnp.int32(1))
@@ -228,83 +346,24 @@
             axis=1,
         )
 
-    def look_up(table, row):
-        row = jnp.maximum(row.astype(jnp.int32), 0)
-        pieces = []
-        for at in range(0, piece, LANES):
-            index = jnp.broadcast_to(row[:, at:at + LANES], (KW, LANES))
-            pieces.append(jnp.take_along_axis(table, index, axis=1))
-        return jnp.concatenate(pieces, axis=1)
-
     lane = lax.broadcasted_iota(jnp.int32, (1, piece), 1)
 
     def make_spread(step, slot):
         keep = lane < jnp.where(
             spot_ref[2 * step + 1] >= 0, piece, jnp.where(spot_ref[2 * step] >= 0, LANES, 0)
         )
-        re = jnp.where(keep, field(step, 0), 0.0)
-        im = jnp.where(keep, field(step, 1), 0.0)
-        v = field(step, 3).astype(jnp.int32)
-        taps_v = look_up(tap_table, field(step, 5))
-        offset = lax.broadcasted_iota(jnp.int32, (SPREAD, piece), 0) - (v & (FINE - 1))
-        spread = jnp.zeros((SPREAD, piece), jnp.float32)
-        for t in range(KW):
-            spread = jnp.where(offset == t, taps_v[t:t + 1, :], spread)
-        both = jnp.concatenate([spread * re, spread * im], axis=0)
-        bh, bl = halves_of(both)
-        pad = jnp.zeros((256 - 6 * SPREAD, piece), jnp.bfloat16)
-        spread_ref[slot] = jnp.concatenate([bh, bh, bl, pad], axis=0)
-        pick = lax.broadcasted_iota(jnp.int32, (2 * coarse_count, piece), 0) & (coarse_count - 1)
-        pick_ref[slot] = jnp.where(pick == v // FINE, 1.0, 0.0).astype(jnp.bfloat16)
+        store_spread(grid, tap_table, lambda n: field(step, n), keep, slot, spread_ref, pick_ref)
 
     def make_z(step, slot):
-        zb = dot(fine_ref[...], spread_ref[slot])
-        e = dot(coarse_ref[...], pick_ref[slot])
-        er, ei = e[:coarse_count], e[coarse_count:]
-        re, im = [], []
-        for at in range(0, cols, coarse_count):
-            zr, zi = zb[at:at + coarse_count], zb[cols + at:cols + at + coarse_count]
-            re.append(zr * er - zi * ei)
-            im.append(zr * ei + zi * er)
-        for n, parts in enumerate((re, im)):
-            zh, zl = halves_of(jnp.concatenate(parts, axis=0).T)
-            z_ref[slot, 0, :, n * cols:(n + 1) * cols] = zh
-            z_ref[slot, 1, :, n * cols:(n + 1) * cols] = zl
-
-        u = field(step, 2).astype(jnp.int32)
-        taps_u = look_up(tap_table, field(step, 4))
-        residue = lax.broadcasted_iota(jnp.int32, (2 * RADIX, piece), 0)
-        tap = (residue - u) & (2 * RADIX - 1)
-        row = lax.shift_right_logical(u + tap, jnp.int32((2 * RADIX).bit_length() - 1))
-        weight = jnp.zeros((2 * RADIX, piece), jnp.float32)
-        for t in range(KW):
-            weight = jnp.where(tap == t, taps_u[t:t + 1, :], weight)
-        high = weight.astype(jnp.bfloat16).astype(jnp.float32)
-        tap_ref[slot, 0] = row.astype(jnp.float32)
-        tap_ref[slot, 1] = high
-        tap_ref[slot, 2] = weight - high
+        store_z(
+            grid, tap_table, lambda n: field(step, n), slot,
+            fine_ref, coarse_ref, spread_ref, pick_ref, z_ref, tap_ref,
+        )
 
     def add_rows(step, slot):
         c = channel_ref[step]
-        rows16 = lax.broadcasted_iota(jnp.int32, (GROUP, piece), 0).astype(jnp.float32)
-        spots = [(rows16 + float(at)).astype(jnp.bfloat16) for at in range(0, half, GROUP)]
-
-        def wide(kind, residue):
-            x = tap_ref[slot, kind, residue:residue + 1, :]
-            return jnp.broadcast_to(x, (GROUP, piece)).astype(jnp.bfloat16)
-
         for first in range(RADIX):
-            highs, lows = [], []
-            for residue in (first, first + RADIX):
-                row, high, low = (wide(kind, residue) for kind in range(3))
-                zero = jnp.zeros_like(high)
-                for spot in spots:
-                    hit = row == spot
-                    highs.append(jnp.where(hit, high, zero))
-                    lows.append(jnp.where(hit, low, zero))
-            wh, wl = jnp.concatenate(highs, axis=0), jnp.concatenate(lows, axis=0)
-            zh, zl = z_ref[slot, 0], z_ref[slot, 1]
-            h_ref[c, first] += dot(wh, zh) + dot(wh, zl) + dot(wl, zh)
+            h_ref[c, first] += slab_of(grid, first, slot, z_ref, tap_ref)
 
     make_spread(0, 0)
     make_z(0, 0)
@@ -321,27 +380,21 @@
     lax.fori_loop(0, (steps + 1) // 2, two_steps, 0)
 
 
-def grid_visibilities(fields, fine, coarse, taps_table, grid):
-    both = fine.shape[0]
+def grid_visibilities(fields, fine, coarse, taps_table, start, grid):
     channels, blocks, rows, _ = fields.shape
     most = channels * (blocks * (rows // FIELDS) + 1)
     smem = lambda n: pltpu.SMEM((n,), jnp.int32)
     vmem = pl.BlockSpec(memory_space=pltpu.VMEM)
     return pl.pallas_call(
         functools.partial(grid_kernel, grid),
-        out_shape=jax.ShapeDtypeStruct((channels, RADIX, grid // RADIX, both), jnp.float32),
-        in_specs=[vmem] * 4,
+        out_shape=jax.ShapeDtypeStruct(start.shape, jnp.float32),
+        in_specs=[vmem] * 5,
         out_specs=vmem,
-        scratch_shapes=[
-            pltpu.VMEM((2, 256, 2 * LANES), jnp.bfloat16),
-            pltpu.VMEM((2, 2 * (grid // FINE), 2 * LANES), jnp.bfloat16),
-            pltpu.VMEM((2, 2, 2 * LANES, both), jnp.bfloat16),
-            pltpu.VMEM((2, 3, 2 * RADIX, 2 * LANES), jnp.float32),
-            smem(most + 16), smem(most // 2 + 16),
-        ],
+        scratch_shapes=step_scratch(grid, start.shape[3]) + [smem(most + 16), smem(most // 2 + 16)],
+        input_output_aliases={4: 0},
         compiler_params=pltpu.CompilerParams(vmem_limit_bytes=16 * 2**20),
         name="grid_visibilities",
-    )(fields, fine, coarse, taps_table)
+    )(fields, fine, coarse, taps_table, start)
 
 
 def power_kernel(
@@ -518,7 +571,7 @@
 
     stage2_ref[base] = share_out(stage_ref, freq, ring, 0)
     total = share_out(stage2_ref, base, line, len(ring))
-    spectrum_ref[...] = total[:lead] / total[lead:]
+    spectrum_ref[...] = total
 
     def finish(n, carry):
         for k in range(RADIX):
@@ -548,7 +601,7 @@
         functools.partial(power_kernel, grid, freq_count, base_count, split, scale),
         out_shape=(
             jax.ShapeDtypeStruct((share_rows, width), f32),
-            jax.ShapeDtypeStruct((4, 4 * BIN_LOW), f32),
+            jax.ShapeDtypeStruct((8, 4 * BIN_LOW), f32),
         ),
         in_specs=[vmem, hbm, hbm, hbm],
         out_specs=(vmem, vmem),
@@ -580,6 +633,28 @@
     )(h, in_hbm(dh), in_hbm(dl), in_hbm(bins))
 
 
+def finish_kernel(share_ref, sums_ref, power_ref, spectrum_ref):
+    power_ref[...] = share_ref[...]
+    mean = sums_ref[0:4, :] / sums_ref[4:8, :]
+    width = mean.shape[1]
+    for n in range(4):
+        spectrum_ref[n * width:(n + 1) * width] = mean[n]
+
+
+def finish(share, sums):
+    vmem = pl.BlockSpec(memory_space=pltpu.VMEM)
+    return pl.pallas_call(
+        finish_kernel,
+        out_shape=(
+            jax.ShapeDtypeStruct(share.shape, share.dtype), jax.ShapeDtypeStruct((NBINS,), jnp.float32)
+        ),
+        in_specs=[vmem, vmem],
+        out_specs=(vmem, vmem),
+        compiler_params=pltpu.CompilerParams(vmem_limit_bytes=4 * 2**20),
+        name="finish",
+    )(share, sums)
+
+
 def per_device(visibility, tile_of, u_within, v_cell, kernel_index, kernel, live_count, bin_map):
     base_count = lax.axis_size("base")
     freq_count = lax.axis_size("freq")
@@ -598,10 +673,10 @@
     bins = bin_map
     if share_rows % LANES:
         bins = lax.dynamic_slice_in_dim(bin_map, lax.axis_index("freq") * share_rows, share_rows, 1)
-    share, spectrum = power_and_spectrum(
+    share, sums = power_and_spectrum(
         h, jnp.asarray(dh), jnp.asarray(dl), bins, grid, freq_count, base_count, split, width, scale
     )
-    return share, spectrum.reshape(NBINS)
+    return finish(share, sums)
 
 
 def solution(mesh):

time: 43.8 us -> 41 us (0.936)
  Pallas kernels: 41.7 us -> 40.1 us
  local copies, waits for them, and re-layouts: 1.24 us -> 0 us
    pallas_call x1, Pallas kernels: 12.9 us -> 9.58 us  [grid_visibilities(): pl.pallas_call(functools.partial(grid_kernel, grid), out_shape=jax.ShapeD...]
    unnamed x2 -> x0, local copies, waits for them, and re-layouts: 1.24 us -> none
    pallas_call x1, Pallas kernels: 19.4 us -> 20.2 us  [power_and_spectrum(): pl.pallas_call(functools.partial(power_kernel, grid, freq_count, base_cou...]
    pallas_call x0 -> x1, Pallas kernels: none -> 0.67 us  [finish(): pl.pallas_call(finish_kernel, out_shape=(jax.ShapeDtypeStruct(share.shape...]
where the time goes in v1:
time: 41 us; the launch traced here: 40.8 us
  Pallas kernels  40.1 us (98%)
  between operations  0.66 us (2%)
    pallas_call x1, Pallas kernels, power_and_spectrum(): pl.pallas_call(functools.partial(power_kernel, grid, freq_count, base_cou...  20.2 us
    pallas_call x1, Pallas kernels, gather_fields(): pl.pallas_call(functools.partial(gather_kernel, split, base_count, tile_r...  9.73 us
    pallas_call x1, Pallas kernels, grid_visibilities(): pl.pallas_call(functools.partial(grid_kernel, grid), out_shape=jax.ShapeD...  9.58 us

profile of v1, /device:TPU:0, one launch (start us, length us, event | category | flops | bytes accessed | tf_op | source)
XLA Modules:
  0.0 40.8 jit_solution(1244220572901079098)
XLA Ops:
  0.6 9.7 %gather_fields.1 = (f32[4,4,24,128]{3,2,1,0:T(8,128)S(1)}, bf16[256,256]{1,0:T(8,128)(2,1)S(1)}, bf16[64,64]{1,0:T(8,128)(2,1)S(1)}, f32[8,128]{1,0:T(8,128)S(1)}, f32[4,4,256,256]{3,2,1,0:T(8,128)S(1)}) custom-call(f32[2,2,512]{2,1,0:T(2,128)} %vis_hbm.1, s32[2,1,512]{2,1,0:T(1,128)} %bitcast.3, s32[2,512]{1,0:T(2,128)} %within_hbm.1, s32[2,512]{1,0:T(2,128)} %column_hbm.1, ...), custom_call_target="tpu_custom_call" | custom-call | tf_op jit(solution)/shard_map/gather_fields/pallas_call | solution.py:281
  10.4 9.6 %grid_visibilities.1.h_ref = f32[4,4,256,256]{3,2,1,0:T(8,128)S(1)} custom-call(f32[4,4,24,128]{3,2,1,0:T(8,128)S(1)} %get-tuple-element.9.f_ref, bf16[256,256]{1,0:T(8,128)(2,1)S(1)} %get-tuple-element.10.fine_ref, bf16[64,64]{1,0:T(8,128)(2,1)S(1)} %get-tuple-element.11.coarse_ref, ...), custom_call_target="tpu_custom_call", output_to_operand_aliasing={{}: (4, {})} | custom-call | tf_op jit(solution)/shard_map/grid_visibilities/pallas_call | solution.py:388
  20.0 20.2 %power_and_spectrum.1 = (f32[128,256]{1,0:T(8,128)S(1)}, f32[8,128]{1,0:T(8,128)S(1)}) custom-call(f32[4,4,256,256]{3,2,1,0:T(8,128)S(1)} %grid_visibilities.1.h_ref, bf16[4,512,256]{2,1,0:T(8,128)(2,1)} %constant.4.clone.dh_hbm, bf16[4,512,256]{2,1,0:T(8,128)(2,1)} %constant.5.clone.dl_hbm, s32[256,1024]{1,0:T(8,128)} %bins_hbm.1), custom_call_target="tpu_custom_call" | custom-call | tf_op jit(solution)/shard_map/power_and_spectrum/pallas_call | solution.py:600
  40.1 0.7 %finish.1 = (f32[128,256]{1,0:T(8,128)}, f32[512]{0:T(512)}) custom-call(f32[128,256]{1,0:T(8,128)S(1)} %get-tuple-element.14.share_ref, f32[8,128]{1,0:T(8,128)S(1)} %get-tuple-element.15.sums_ref), custom_call_target="tpu_custom_call" | custom-call | tf_op jit(solution)/shard_map/finish/pallas_call | solution.py:646

commit v2 on v1

--- a/solution.py
+++ b/solution.py
@@ -178,6 +178,12 @@
         pltpu.VMEM((2, 2, piece, both), bf16),
         pltpu.VMEM((2, 3, 2 * RADIX, piece), f32),
     ]
+
+
+def second_pair(base, subs):
+    if subs < 4:
+        return lax.rem(base + lax.axis_size("base") - 1, lax.axis_size("base")), 0
+    return jnp.maximum(base - 1, 0), jnp.where(base == 0, 2, 0)
 
 
 def gather_kernel(
@@ -243,14 +249,13 @@
     pass_on(0)
     subs = slots // LANES
     table = taps_ref[...]
-    for d in range(split):
-        if d:
-            passed[split - 1 - d][0].wait_recv()
+
+    def grid_group(d, owner, sub, begin):
         group = lax.rem(part + d, split) * channels
 
         def field_of(c):
             def field(number):
-                rows = [out_ref[group + c, base, pl.ds(number * subs + n, 1), :] for n in range(2)]
+                rows = [out_ref[group + c, owner, pl.ds(number * subs + sub + n, 1), :] for n in range(2)]
                 return jnp.concatenate(rows, axis=1)
             return field
 
@@ -258,14 +263,28 @@
             store_spread(grid, table, field_of(c), None, c % 2, spread_ref, pick_ref)
             store_z(grid, table, field_of(c), c % 2, fine_ref, coarse_ref, spread_ref, pick_ref, z_ref, tap_ref)
             for residue in range(RADIX):
-                h_ref[group + c, residue] = slab_of(grid, residue, c % 2, z_ref, tap_ref)
+                rows = slab_of(grid, residue, c % 2, z_ref, tap_ref)
+                h_ref[group + c, residue] = rows if begin else h_ref[group + c, residue] + rows
+
+    grid_group(0, base, 0, True)
+    for d in range(1, split):
+        passed[split - 1 - d][0].wait_recv()
+        grid_group(d, base, 0, True)
+    below, sub = second_pair(base, subs)
     for d in range(1, base_count):
+        if d == base_count - 1 and d > 1:
+            grid_group(0, below, sub, False)
         sent[d - 1].wait_recv()
         pass_on(d)
+    if base_count < 3:
+        grid_group(0, below, sub, False)
+    for d in range(1, split):
+        passed[split - 1 - d][1].wait_recv()
+        grid_group(d, below, sub, False)
     for k in range(len(mates)):
         for d, copy in enumerate(passed[k]):
             copy.wait_send()
-            if d:
+            if d > 1:
                 copy.wait_recv()
     for copy in sent:
         copy.wait_send()
@@ -309,6 +328,7 @@
     piece = 2 * LANES
     tap_table = kernel_ref[...]
     base = lax.axis_index("base")
+    below, _ = second_pair(base, subs)
 
     counts = []
     for c in range(channels):
@@ -318,7 +338,7 @@
     filled = jnp.int32(0)
     for c in range(channels):
         for b in range(blocks):
-            done = jnp.where(base == b, 2, 0)
+            done = jnp.where(base == b, 2, 0) + jnp.where(below == b, 2, 0)
             for sub in range(subs):
                 spot_ref[filled + sub] = b * subs + sub + done
             for ahead in range(subs // 2 + 1):

time: 41 us -> 41 us (level); the launches traced: 40.8 us -> 41.2 us
  Pallas kernels: 40.1 us -> 40.6 us
    pallas_call x1, Pallas kernels: 9.73 us -> 12.3 us  [gather_fields(): pl.pallas_call(functools.partial(gather_kernel, split, base_count, tile_r...]
    pallas_call x1, Pallas kernels: 20.2 us -> 18 us  [power_and_spectrum(): pl.pallas_call(functools.partial(power_kernel, grid, freq_count, base_cou...]
where the time goes in v2:
time: 41 us; the launch traced here: 41.2 us
  Pallas kernels  40.6 us (99%)
  between operations  0.66 us (2%)
    pallas_call x1, Pallas kernels, power_and_spectrum(): pl.pallas_call(functools.partial(power_kernel, grid, freq_count, base_cou...  18 us
    pallas_call x1, Pallas kernels, gather_fields(): pl.pallas_call(functools.partial(gather_kernel, split, base_count, tile_r...  12.3 us
    pallas_call x1, Pallas kernels, grid_visibilities(): pl.pallas_call(functools.partial(grid_kernel, grid), out_shape=jax.ShapeD...  9.58 us

profile of v2, /device:TPU:0, one launch (start us, length us, event | category | flops | bytes accessed | tf_op | source)
XLA Modules:
  0.0 41.2 jit_solution(11930050997961755124)
XLA Ops:
  0.6 12.3 %gather_fields.1 = (f32[4,4,24,128]{3,2,1,0:T(8,128)S(1)}, bf16[256,256]{1,0:T(8,128)(2,1)S(1)}, bf16[64,64]{1,0:T(8,128)(2,1)S(1)}, f32[8,128]{1,0:T(8,128)S(1)}, f32[4,4,256,256]{3,2,1,0:T(8,128)S(1)}) custom-call(f32[2,2,512]{2,1,0:T(2,128)} %vis_hbm.1, s32[2,1,512]{2,1,0:T(1,128)} %bitcast.3, s32[2,512]{1,0:T(2,128)} %within_hbm.1, s32[2,512]{1,0:T(2,128)} %column_hbm.1, ...), custom_call_target="tpu_custom_call" | custom-call | tf_op jit(solution)/shard_map/gather_fields/pallas_call | solution.py:300
  13.0 9.6 %grid_visibilities.1.h_ref = f32[4,4,256,256]{3,2,1,0:T(8,128)S(1)} custom-call(f32[4,4,24,128]{3,2,1,0:T(8,128)S(1)} %get-tuple-element.9.f_ref, bf16[256,256]{1,0:T(8,128)(2,1)S(1)} %get-tuple-element.10.fine_ref, bf16[64,64]{1,0:T(8,128)(2,1)S(1)} %get-tuple-element.11.coarse_ref, ...), custom_call_target="tpu_custom_call", output_to_operand_aliasing={{}: (4, {})} | custom-call | tf_op jit(solution)/shard_map/grid_visibilities/pallas_call | solution.py:408
  22.6 18.0 %power_and_spectrum.1 = (f32[128,256]{1,0:T(8,128)S(1)}, f32[8,128]{1,0:T(8,128)S(1)}) custom-call(f32[4,4,256,256]{3,2,1,0:T(8,128)S(1)} %grid_visibilities.1.h_ref, bf16[4,512,256]{2,1,0:T(8,128)(2,1)} %constant.4.clone.dh_hbm, bf16[4,512,256]{2,1,0:T(8,128)(2,1)} %constant.5.clone.dl_hbm, s32[256,1024]{1,0:T(8,128)} %bins_hbm.1), custom_call_target="tpu_custom_call" | custom-call | tf_op jit(solution)/shard_map/power_and_spectrum/pallas_call | solution.py:620
  40.6 0.7 %finish.1 = (f32[128,256]{1,0:T(8,128)}, f32[512]{0:T(512)}) custom-call(f32[128,256]{1,0:T(8,128)S(1)} %get-tuple-element.14.share_ref, f32[8,128]{1,0:T(8,128)S(1)} %get-tuple-element.15.sums_ref), custom_call_target="tpu_custom_call" | custom-call | tf_op jit(solution)/shard_map/finish/pallas_call | solution.py:666

commit v3 on v2

--- a/solution.py
+++ b/solution.py
@@ -18,6 +18,9 @@
 GROUP = 16
 FIELDS = 6
 LANES = 128
+F8 = jnp.float8_e5m2
+Z_SCALE = 2.0 ** 9
+W_SCALE = 2.0 ** 12
 MESH = pl.DeviceIdType.MESH
 
 
@@ -108,6 +111,7 @@
     spread = jnp.zeros((SPREAD, piece), jnp.float32)
     for t in range(KW):
         spread = jnp.where(offset == t, taps_v[t:t + 1, :], spread)
+    re, im = re * Z_SCALE, im * Z_SCALE
     both = jnp.concatenate([spread * re, spread * im], axis=0)
     bh, bl = halves_of(both)
     pad = jnp.zeros((256 - 6 * SPREAD, piece), jnp.bfloat16)
@@ -116,7 +120,7 @@
     pick_ref[slot] = jnp.where(pick == v // FINE, 1.0, 0.0).astype(jnp.bfloat16)
 
 
-def store_z(grid, table, field, slot, fine_ref, coarse_ref, spread_ref, pick_ref, z_ref, tap_ref):
+def store_z(grid, table, field, slot, fine_ref, coarse_ref, spread_ref, pick_ref, z_ref, z8_ref, tap_ref):
     cols = fine_ref.shape[0] // 2
     coarse_count = grid // FINE
     zb = dot(fine_ref[...], spread_ref[slot])
@@ -128,9 +132,11 @@
         re.append(zr * er - zi * ei)
         im.append(zr * ei + zi * er)
     for n, parts in enumerate((re, im)):
-        zh, zl = halves_of(jnp.concatenate(parts, axis=0).T)
+        turned = jnp.concatenate(parts, axis=0).T
+        zh, zl = halves_of(turned)
         z_ref[slot, 0, :, n * cols:(n + 1) * cols] = zh
         z_ref[slot, 1, :, n * cols:(n + 1) * cols] = zl
+        z8_ref[slot, :, n * cols:(n + 1) * cols] = turned.astype(F8)
 
     u = field(2).astype(jnp.int32)
     taps_u = look_up(table, field(4))
@@ -140,13 +146,14 @@
     weight = jnp.zeros(tap.shape, jnp.float32)
     for t in range(KW):
         weight = jnp.where(tap == t, taps_u[t:t + 1, :], weight)
+    weight = weight * W_SCALE
     high = weight.astype(jnp.bfloat16).astype(jnp.float32)
     tap_ref[slot, 0] = row.astype(jnp.float32)
     tap_ref[slot, 1] = high
     tap_ref[slot, 2] = weight - high
 
 
-def slab_of(grid, first, slot, z_ref, tap_ref):
+def slab_of(grid, first, slot, z_ref, z8_ref, tap_ref):
     half = grid // (2 * RADIX)
     piece = tap_ref.shape[3]
     rows16 = lax.broadcasted_iota(jnp.int32, (GROUP, piece), 0).astype(jnp.float32)
@@ -166,7 +173,7 @@
             lows.append(jnp.where(hit, low, zero))
     wh, wl = jnp.concatenate(highs, axis=0), jnp.concatenate(lows, axis=0)
     zh, zl = z_ref[slot, 0], z_ref[slot, 1]
-    return dot(wh, zh) + dot(wh, zl) + dot(wl, zh)
+    return dot(wh, zh) + dot(wh, zl) + dot(wl.astype(F8), z8_ref[slot])
 
 
 def step_scratch(grid, both):
@@ -176,6 +183,7 @@
         pltpu.VMEM((2, 256, piece), bf16),
         pltpu.VMEM((2, 2 * (grid // FINE), piece), bf16),
         pltpu.VMEM((2, 2, piece, both), bf16),
+        pltpu.VMEM((2, piece, both), F8),
         pltpu.VMEM((2, 3, 2 * RADIX, piece), f32),
     ]
 
@@ -190,7 +198,7 @@
     split, base_count, tile_rows, grid, vis_hbm, tile_hbm, within_hbm, column_hbm, index_hbm, live_hbm,
     taps_hbm, out_ref, fine_ref, coarse_ref, taps_ref, h_ref,
     vis_ref, tile_ref, within_ref, column_ref, index_ref, live_ref, load_sems, send_sems, recv_sems,
-    spread_ref, pick_ref, z_ref, tap_ref
+    spread_ref, pick_ref, z_ref, z8_ref, tap_ref
 ):
     freq, base = lax.axis_index("freq"), lax.axis_index("base")
     part = lax.rem(freq, split)
@@ -261,9 +269,9 @@
 
         for c in range(channels):
             store_spread(grid, table, field_of(c), None, c % 2, spread_ref, pick_ref)
-            store_z(grid, table, field_of(c), c % 2, fine_ref, coarse_ref, spread_ref, pick_ref, z_ref, tap_ref)
+            store_z(grid, table, field_of(c), c % 2, fine_ref, coarse_ref, spread_ref, pick_ref, z_ref, z8_ref, tap_ref)
             for residue in range(RADIX):
-                rows = slab_of(grid, residue, c % 2, z_ref, tap_ref)
+                rows = slab_of(grid, residue, c % 2, z_ref, z8_ref, tap_ref)
                 h_ref[group + c, residue] = rows if begin else h_ref[group + c, residue] + rows
 
     grid_group(0, base, 0, True)
@@ -320,9 +328,15 @@
 
 
 def grid_kernel(
-    grid, f_ref, fine_ref, coarse_ref, kernel_ref, start_ref, h_ref,
-    spread_ref, pick_ref, z_ref, tap_ref, spot_ref, channel_ref
+    grid, f_ref, fine_ref, coarse_ref, kernel_ref, start_ref, dh_hbm, dl_hbm, h_ref, dh_ref, dl_ref,
+    spread_ref, pick_ref, z_ref, z8_ref, tap_ref, spot_ref, channel_ref, load_sems
 ):
+    loads = []
+    for n in range(RADIX):
+        loads.append(pltpu.make_async_copy(dh_hbm.at[n], dh_ref.at[n], load_sems.at[0, n]))
+        loads.append(pltpu.make_async_copy(dl_hbm.at[n], dl_ref.at[n], load_sems.at[1, n]))
+    for load in loads:
+        load.start()
     channels, blocks, rows, _ = f_ref.shape
     subs = rows // FIELDS
     piece = 2 * LANES
@@ -377,13 +391,13 @@
     def make_z(step, slot):
         store_z(
             grid, tap_table, lambda n: field(step, n), slot,
-            fine_ref, coarse_ref, spread_ref, pick_ref, z_ref, tap_ref,
+            fine_ref, coarse_ref, spread_ref, pick_ref, z_ref, z8_ref, tap_ref,
         )
 
     def add_rows(step, slot):
         c = channel_ref[step]
         for first in range(RADIX):
-            h_ref[c, first] += slab_of(grid, first, slot, z_ref, tap_ref)
+            h_ref[c, first] += slab_of(grid, first, slot, z_ref, z8_ref, tap_ref)
 
     make_spread(0, 0)
     make_z(0, 0)
@@ -393,45 +407,48 @@
         for slot in range(2):
             step = 2 * n + slot
             make_z(step + 1, 1 - slot)
+            make_spread(step + 2, slot)
             add_rows(step, slot)
-            make_spread(step + 2, slot)
         return carry
 
     lax.fori_loop(0, (steps + 1) // 2, two_steps, 0)
-
-
-def grid_visibilities(fields, fine, coarse, taps_table, start, grid):
+    for load in loads:
+        load.wait()
+
+
+def grid_visibilities(fields, fine, coarse, taps_table, start, dh, dl, grid):
     channels, blocks, rows, _ = fields.shape
     most = channels * (blocks * (rows // FIELDS) + 1)
     smem = lambda n: pltpu.SMEM((n,), jnp.int32)
     vmem = pl.BlockSpec(memory_space=pltpu.VMEM)
+    hbm = pl.BlockSpec(memory_space=pltpu.HBM)
     return pl.pallas_call(
         functools.partial(grid_kernel, grid),
-        out_shape=jax.ShapeDtypeStruct(start.shape, jnp.float32),
-        in_specs=[vmem] * 5,
-        out_specs=vmem,
-        scratch_shapes=step_scratch(grid, start.shape[3]) + [smem(most + 16), smem(most // 2 + 16)],
+        out_shape=(
+            jax.ShapeDtypeStruct(start.shape, jnp.float32),
+            jax.ShapeDtypeStruct(dh.shape, jnp.bfloat16),
+            jax.ShapeDtypeStruct(dl.shape, jnp.bfloat16),
+        ),
+        in_specs=[vmem] * 5 + [hbm] * 2,
+        out_specs=(vmem,) * 3,
+        scratch_shapes=step_scratch(grid, start.shape[3]) + [
+            smem(most + 16), smem(most // 2 + 16), pltpu.SemaphoreType.DMA((2, RADIX)),
+        ],
         input_output_aliases={4: 0},
         compiler_params=pltpu.CompilerParams(vmem_limit_bytes=16 * 2**20),
         name="grid_visibilities",
-    )(fields, fine, coarse, taps_table, start)
+    )(fields, fine, coarse, taps_table, start, in_hbm(dh), in_hbm(dl))
 
 
 def power_kernel(
-    grid, freq_count, base_count, split, scale, h_ref, dh_hbm, dl_hbm, bins_hbm, share_ref, spectrum_ref,
-    dh_ref, dl_ref, bins_ref, load_sems, bins_sem, hh_ref, hl_ref, y_ref, power_ref, recv_ref, mask_ref, value_ref, low_ref, stage_ref, stage2_ref,
+    grid, freq_count, base_count, split, scale, h_ref, dh_ref, dl_ref, bins_hbm, share_ref, spectrum_ref,
+    bins_ref, bins_sem, hh_ref, hl_ref, y_ref, power_ref, recv_ref, mask_ref, value_ref, low_ref, stage_ref, stage2_ref,
     send_sems, recv_sems, sum_send_sems, sum_recv_sems
 ):
     freq, base = lax.axis_index("freq"), lax.axis_index("base")
     ring = [{"freq": lax.rem(freq + d, freq_count), "base": base} for d in range(1, freq_count)]
     line = [{"freq": freq, "base": lax.rem(base + d, base_count)} for d in range(1, base_count)]
     barrier = greet(ring + line)
-    loads = []
-    for n in range(RADIX):
-        loads.append(pltpu.make_async_copy(dh_hbm.at[n], dh_ref.at[n], load_sems.at[0, n]))
-        loads.append(pltpu.make_async_copy(dl_hbm.at[n], dl_ref.at[n], load_sems.at[1, n]))
-    for load in loads:
-        load.start()
     rows_here = bins_ref.shape[1]
     if bins_hbm.shape[1] != rows_here:
         here = pl.ds(pl.multiple_of(freq * rows_here, rows_here), rows_here)
@@ -448,17 +465,7 @@
     parts = share_rows // chunk
     shares = slab // share_rows
 
-    def split_rows(n, carry):
-        high, low = halves_of(h_ref[n // RADIX, n % RADIX])
-        hh_ref[n // RADIX, n % RADIX] = high
-        hl_ref[n // RADIX, n % RADIX] = low
-        return carry
-
-    lax.fori_loop(0, channels * RADIX, split_rows, 0)
-    for load in loads:
-        load.wait()
-
-    def transform(n):
+    def transform(n, begin=False):
         top = pl.multiple_of((lax.rem(n, shares) * parts + n // shares) * chunk, chunk)
         for c in range(channels):
             for first in range(RADIX):
@@ -468,7 +475,12 @@
                 dl = jnp.concatenate(
                     [dl_ref[first, pl.ds(top, chunk), :], dl_ref[first, pl.ds(slab + top, chunk), :]], axis=0
                 )
-                hh, hl = hh_ref[c, first], hl_ref[c, first]
+                if begin:
+                    hh, hl = halves_of(h_ref[c, first])
+                    hh_ref[c, first] = hh
+                    hl_ref[c, first] = hl
+                else:
+                    hh, hl = hh_ref[c, first], hl_ref[c, first]
                 y_ref[c % 2, first] = dot(dh, hh) + dot(dl, hh) + dot(dh, hl)
             step = min(16, chunk)
             for row in range(0, chunk, step):
@@ -515,7 +527,7 @@
             def _():
                 copy.start()
 
-    transform(0)
+    transform(0, True)
     pl.semaphore_wait(barrier, len(ring) + len(line))
     send(0)
 
@@ -623,13 +635,10 @@
             jax.ShapeDtypeStruct((share_rows, width), f32),
             jax.ShapeDtypeStruct((8, 4 * BIN_LOW), f32),
         ),
-        in_specs=[vmem, hbm, hbm, hbm],
+        in_specs=[vmem, vmem, vmem, hbm],
         out_specs=(vmem, vmem),
         scratch_shapes=[
-            pltpu.VMEM(dh.shape, bf16),
-            pltpu.VMEM(dl.shape, bf16),
             pltpu.VMEM((bins.shape[0], share_rows), jnp.int32),
-            pltpu.SemaphoreType.DMA((2, RADIX)),
             pltpu.SemaphoreType.DMA,
             pltpu.VMEM(h.shape, bf16),
             pltpu.VMEM(h.shape, bf16),
@@ -650,7 +659,7 @@
             collective_id=1, has_side_effects=True, vmem_limit_bytes=24 * 2**20
         ),
         name="power_and_spectrum",
-    )(h, in_hbm(dh), in_hbm(dl), in_hbm(bins))
+    )(h, dh, dl, in_hbm(bins))
 
 
 def finish_kernel(share_ref, sums_ref, power_ref, spectrum_ref):
@@ -683,18 +692,18 @@
     split = 2 if width % (2 * LANES) == 0 and freq_count % 2 == 0 else 1
     channels_here, slots = u_within.shape
     dh, dl = transform_tables(grid)
-    scale = 1.0 / (channels_here * freq_count * slots * base_count)
+    scale = 1.0 / (channels_here * freq_count * slots * base_count) / (Z_SCALE * W_SCALE) ** 2
     gathered = gather_fields(
         split, base_count, grid // base_count, grid, width // split,
         visibility, tile_of.transpose(0, 2, 1), u_within, v_cell, kernel_index, live_count.T, kernel.T,
     )
-    h = grid_visibilities(*gathered, grid)
+    h, dh, dl = grid_visibilities(*gathered, jnp.asarray(dh), jnp.asarray(dl), grid)
     share_rows = grid // freq_count
     bins = bin_map
     if share_rows % LANES:
         bins = lax.dynamic_slice_in_dim(bin_map, lax.axis_index("freq") * share_rows, share_rows, 1)
     share, sums = power_and_spectrum(
-        h, jnp.asarray(dh), jnp.asarray(dl), bins, grid, freq_count, base_count, split, width, scale
+        h, dh, dl, bins, grid, freq_count, base_count, split, width, scale
     )
     return finish(share, sums)
 

time: 41 us -> 40.3 us (0.983)
  Pallas kernels: 40.6 us -> 40 us
    pallas_call x1, Pallas kernels: 9.58 us -> 6.09 us  [grid_visibilities(): pl.pallas_call(functools.partial(grid_kernel, grid), out_shape=(jax.Shape...]
    pallas_call x1, Pallas kernels: 18 us -> 21.3 us  [power_and_spectrum(): pl.pallas_call(functools.partial(power_kernel, grid, freq_count, base_cou...]
    pallas_call x1, Pallas kernels: 12.3 us -> 11.9 us  [gather_fields(): pl.pallas_call(functools.partial(gather_kernel, split, base_count, tile_r...]
where the time goes in v3:
time: 40.3 us; the launch traced here: 40.6 us
  Pallas kernels  40 us (99%)
  between operations  0.66 us (2%)
    pallas_call x1, Pallas kernels, power_and_spectrum(): pl.pallas_call(functools.partial(power_kernel, grid, freq_count, base_cou...  21.3 us
    pallas_call x1, Pallas kernels, gather_fields(): pl.pallas_call(functools.partial(gather_kernel, split, base_count, tile_r...  11.9 us
    pallas_call x1, Pallas kernels, grid_visibilities(): pl.pallas_call(functools.partial(grid_kernel, grid), out_shape=(jax.Shape...  6.09 us

profile of v3, /device:TPU:0, one launch (start us, length us, event | category | flops | bytes accessed | tf_op | source)
XLA Modules:
  0.0 40.6 jit_solution(8445849820736019638)
XLA Ops:
  0.6 11.9 %gather_fields.1 = (f32[4,4,24,128]{3,2,1,0:T(8,128)S(1)}, bf16[256,256]{1,0:T(8,128)(2,1)S(1)}, bf16[64,64]{1,0:T(8,128)(2,1)S(1)}, f32[8,128]{1,0:T(8,128)S(1)}, f32[4,4,256,256]{3,2,1,0:T(8,128)S(1)}) custom-call(f32[2,2,512]{2,1,0:T(2,128)} %vis_hbm.1, s32[2,1,512]{2,1,0:T(1,128)} %bitcast.3, s32[2,512]{1,0:T(2,128)} %within_hbm.1, s32[2,512]{1,0:T(2,128)} %column_hbm.1, ...), custom_call_target="tpu_custom_call" | custom-call | tf_op jit(solution)/shard_map/gather_fields/pallas_call | solution.py:308
  12.5 6.1 %grid_visibilities.1 = (f32[4,4,256,256]{3,2,1,0:T(8,128)S(1)}, bf16[4,512,256]{2,1,0:T(8,128)(2,1)S(1)}, bf16[4,512,256]{2,1,0:T(8,128)(2,1)S(1)}) custom-call(f32[4,4,24,128]{3,2,1,0:T(8,128)S(1)} %get-tuple-element.12.f_ref, bf16[256,256]{1,0:T(8,128)(2,1)S(1)} %get-tuple-element.13.fine_ref, ...), custom_call_target="tpu_custom_call", output_to_operand_aliasing={{0}: (4, {})} | custom-call | tf_op jit(solution)/shard_map/grid_visibilities/pallas_call | solution.py:425
  18.6 21.3 %power_and_spectrum.1 = (f32[128,256]{1,0:T(8,128)S(1)}, f32[8,128]{1,0:T(8,128)S(1)}) custom-call(f32[4,4,256,256]{3,2,1,0:T(8,128)S(1)} %get-tuple-element.17.h_ref, bf16[4,512,256]{2,1,0:T(8,128)(2,1)S(1)} %get-tuple-element.18.dh_ref, bf16[4,512,256]{2,1,0:T(8,128)(2,1)S(1)} %get-tuple-element.19.dl_ref, s32[256,1024]{1,0:T(8,128)} %bins_hbm.1), custom_call_target="tpu_custom_call" | custom-call | tf_op jit(solution)/shard_map/power_and_spectrum/pallas_call | solution.py:632
  39.9 0.7 %finish.1 = (f32[128,256]{1,0:T(8,128)}, f32[512]{0:T(512)}) custom-call(f32[128,256]{1,0:T(8,128)S(1)} %get-tuple-element.20.share_ref, f32[8,128]{1,0:T(8,128)S(1)} %get-tuple-element.21.sums_ref), custom_call_target="tpu_custom_call" | custom-call | tf_op jit(solution)/shard_map/finish/pallas_call | solution.py:675

commit v4 on v3

--- a/solution.py
+++ b/solution.py
@@ -19,8 +19,10 @@
 FIELDS = 6
 LANES = 128
 F8 = jnp.float8_e5m2
+F8W = jnp.float8_e4m3fn
 Z_SCALE = 2.0 ** 9
 W_SCALE = 2.0 ** 12
+LIFT = 2.0 ** 9
 MESH = pl.DeviceIdType.MESH
 
 
@@ -123,6 +125,7 @@
 def store_z(grid, table, field, slot, fine_ref, coarse_ref, spread_ref, pick_ref, z_ref, z8_ref, tap_ref):
     cols = fine_ref.shape[0] // 2
     coarse_count = grid // FINE
+    piece = z_ref.shape[1]
     zb = dot(fine_ref[...], spread_ref[slot])
     e = dot(coarse_ref[...], pick_ref[slot])
     er, ei = e[:coarse_count], e[coarse_count:]
@@ -133,10 +136,11 @@
         im.append(zr * ei + zi * er)
     for n, parts in enumerate((re, im)):
         turned = jnp.concatenate(parts, axis=0).T
-        zh, zl = halves_of(turned)
-        z_ref[slot, 0, :, n * cols:(n + 1) * cols] = zh
-        z_ref[slot, 1, :, n * cols:(n + 1) * cols] = zl
-        z8_ref[slot, :, n * cols:(n + 1) * cols] = turned.astype(F8)
+        zh = turned.astype(jnp.bfloat16)
+        zl = turned - zh.astype(jnp.float32)
+        z_ref[slot, :, n * cols:(n + 1) * cols] = zh
+        z8_ref[slot, 0:piece, n * cols:(n + 1) * cols] = turned.astype(F8)
+        z8_ref[slot, piece:, n * cols:(n + 1) * cols] = (zl * LIFT).astype(F8)
 
     u = field(2).astype(jnp.int32)
     taps_u = look_up(table, field(4))
@@ -151,6 +155,7 @@
     tap_ref[slot, 0] = row.astype(jnp.float32)
     tap_ref[slot, 1] = high
     tap_ref[slot, 2] = weight - high
+    tap_ref[slot, 3] = high * (1.0 / LIFT)
 
 
 def slab_of(grid, first, slot, z_ref, z8_ref, tap_ref):
@@ -163,17 +168,18 @@
         x = tap_ref[slot, kind, residue:residue + 1, :]
         return jnp.broadcast_to(x, (GROUP, piece)).astype(jnp.bfloat16)
 
-    highs, lows = [], []
+    highs, lows, shifts = [], [], []
     for residue in (first, first + RADIX):
-        row, high, low = (wide(kind, residue) for kind in range(3))
+        row, high, low, shift = (wide(kind, residue) for kind in range(4))
         zero = jnp.zeros_like(high)
         for spot in spots:
             hit = row == spot
             highs.append(jnp.where(hit, high, zero))
             lows.append(jnp.where(hit, low, zero))
-    wh, wl = jnp.concatenate(highs, axis=0), jnp.concatenate(lows, axis=0)
-    zh, zl = z_ref[slot, 0], z_ref[slot, 1]
-    return dot(wh, zh) + dot(wh, zl) + dot(wl.astype(F8), z8_ref[slot])
+            shifts.append(jnp.where(hit, shift, zero))
+    wh = jnp.concatenate(highs, axis=0)
+    small = [jnp.concatenate(x, axis=0).astype(F8W) for x in (lows, shifts)]
+    return dot(wh, z_ref[slot]) + dot(jnp.concatenate(small, axis=1), z8_ref[slot])
 
 
 def step_scratch(grid, both):
@@ -182,9 +188,9 @@
     return [
         pltpu.VMEM((2, 256, piece), bf16),
         pltpu.VMEM((2, 2 * (grid // FINE), piece), bf16),
-        pltpu.VMEM((2, 2, piece, both), bf16),
-        pltpu.VMEM((2, piece, both), F8),
-        pltpu.VMEM((2, 3, 2 * RADIX, piece), f32),
+        pltpu.VMEM((2, piece, both), bf16),
+        pltpu.VMEM((2, 2 * piece, both), F8),
+        pltpu.VMEM((2, 4, 2 * RADIX, piece), f32),
     ]
 
 

time: 40.3 us -> 39 us (0.968); the launches traced: 40.6 us -> 38.8 us
  Pallas kernels: 40 us -> 38.1 us
    pallas_call x1, Pallas kernels: 21.3 us -> 20.5 us  [power_and_spectrum(): pl.pallas_call(functools.partial(power_kernel, grid, freq_count, base_cou...]
    pallas_call x1, Pallas kernels: 11.9 us -> 11.4 us  [gather_fields(): pl.pallas_call(functools.partial(gather_kernel, split, base_count, tile_r...]
    pallas_call x1, Pallas kernels: 6.09 us -> 5.59 us  [grid_visibilities(): pl.pallas_call(functools.partial(grid_kernel, grid), out_shape=(jax.Shape...]
where the time goes in v4:
time: 39 us; the launch traced here: 38.8 us
  Pallas kernels  38.1 us (98%)
  between operations  0.66 us (2%)
    pallas_call x1, Pallas kernels, power_and_spectrum(): pl.pallas_call(functools.partial(power_kernel, grid, freq_count, base_cou...  20.5 us
    pallas_call x1, Pallas kernels, gather_fields(): pl.pallas_call(functools.partial(gather_kernel, split, base_count, tile_r...  11.4 us
    pallas_call x1, Pallas kernels, grid_visibilities(): pl.pallas_call(functools.partial(grid_kernel, grid), out_shape=(jax.Shape...  5.59 us

profile of v4, /device:TPU:0, one launch (start us, length us, event | category | flops | bytes accessed | tf_op | source)
XLA Modules:
  0.0 38.8 jit_solution(12699975804112549922)
XLA Ops:
  0.6 11.4 %gather_fields.1 = (f32[4,4,24,128]{3,2,1,0:T(8,128)S(1)}, bf16[256,256]{1,0:T(8,128)(2,1)S(1)}, bf16[64,64]{1,0:T(8,128)(2,1)S(1)}, f32[8,128]{1,0:T(8,128)S(1)}, f32[4,4,256,256]{3,2,1,0:T(8,128)S(1)}) custom-call(f32[2,2,512]{2,1,0:T(2,128)} %vis_hbm.1, s32[2,1,512]{2,1,0:T(1,128)} %bitcast.3, s32[2,512]{1,0:T(2,128)} %within_hbm.1, s32[2,512]{1,0:T(2,128)} %column_hbm.1, ...), custom_call_target="tpu_custom_call" | custom-call | tf_op jit(solution)/shard_map/gather_fields/pallas_call | solution.py:314
  12.0 5.6 %grid_visibilities.1 = (f32[4,4,256,256]{3,2,1,0:T(8,128)S(1)}, bf16[4,512,256]{2,1,0:T(8,128)(2,1)S(1)}, bf16[4,512,256]{2,1,0:T(8,128)(2,1)S(1)}) custom-call(f32[4,4,24,128]{3,2,1,0:T(8,128)S(1)} %get-tuple-element.12.f_ref, bf16[256,256]{1,0:T(8,128)(2,1)S(1)} %get-tuple-element.13.fine_ref, ...), custom_call_target="tpu_custom_call", output_to_operand_aliasing={{0}: (4, {})} | custom-call | tf_op jit(solution)/shard_map/grid_visibilities/pallas_call | solution.py:431
  17.6 20.5 %power_and_spectrum.1 = (f32[128,256]{1,0:T(8,128)S(1)}, f32[8,128]{1,0:T(8,128)S(1)}) custom-call(f32[4,4,256,256]{3,2,1,0:T(8,128)S(1)} %get-tuple-element.17.h_ref, bf16[4,512,256]{2,1,0:T(8,128)(2,1)S(1)} %get-tuple-element.18.dh_ref, bf16[4,512,256]{2,1,0:T(8,128)(2,1)S(1)} %get-tuple-element.19.dl_ref, s32[256,1024]{1,0:T(8,128)} %bins_hbm.1), custom_call_target="tpu_custom_call" | custom-call | tf_op jit(solution)/shard_map/power_and_spectrum/pallas_call | solution.py:638
  38.1 0.7 %finish.1 = (f32[128,256]{1,0:T(8,128)}, f32[512]{0:T(512)}) custom-call(f32[128,256]{1,0:T(8,128)S(1)} %get-tuple-element.20.share_ref, f32[8,128]{1,0:T(8,128)S(1)} %get-tuple-element.21.sums_ref), custom_call_target="tpu_custom_call" | custom-call | tf_op jit(solution)/shard_map/finish/pallas_call | solution.py:681

commit v5 on v4

--- a/solution.py
+++ b/solution.py
@@ -75,8 +75,9 @@
     cols = fine_ref.shape[0] // 2
     coarse_count = grid // FINE
     left = (lax.axis_index("base") * split + lax.rem(lax.axis_index("freq"), split)) * cols
-    l = left + lax.broadcasted_iota(jnp.int32, (cols, SPREAD), 0)
-    c, s = phase(l * lax.broadcasted_iota(jnp.int32, (cols, SPREAD), 1), grid)
+    l = left + lax.broadcasted_iota(jnp.int32, (SPREAD, cols), 1)
+    c, s = phase(l * lax.broadcasted_iota(jnp.int32, (SPREAD, cols), 0), grid)
+    c, s = c.T, s.T
     fine = jnp.concatenate(
         [jnp.concatenate([c, s], axis=1), jnp.concatenate([-s, c], axis=1)], axis=0
     )
@@ -417,7 +418,12 @@
             add_rows(step, slot)
         return carry
 
-    lax.fori_loop(0, (steps + 1) // 2, two_steps, 0)
+    lax.fori_loop(0, lax.shift_right_logical(steps, jnp.int32(1)), two_steps, 0)
+
+    @pl.when((steps & 1) == 1)
+    def _():
+        add_rows(steps - 1, 0)
+
     for load in loads:
         load.wait()
 

time: 39 us -> 38.7 us (level)
  no operation moved by 1% of the time
where the time goes in v5:
time: 38.7 us; the launch traced here: 38.5 us
  Pallas kernels  37.8 us (98%)
  between operations  0.66 us (2%)
    pallas_call x1, Pallas kernels, power_and_spectrum(): pl.pallas_call(functools.partial(power_kernel, grid, freq_count, base_cou...  20.3 us
    pallas_call x1, Pallas kernels, gather_fields(): pl.pallas_call(functools.partial(gather_kernel, split, base_count, tile_r...  11.3 us
    pallas_call x1, Pallas kernels, grid_visibilities(): pl.pallas_call(functools.partial(grid_kernel, grid), out_shape=(jax.Shape...  5.58 us

profile of v5, /device:TPU:0, one launch (start us, length us, event | category | flops | bytes accessed | tf_op | source)
XLA Modules:
  0.0 38.5 jit_solution(8904481222465509335)
XLA Ops:
  0.6 11.3 %gather_fields.1 = (f32[4,4,24,128]{3,2,1,0:T(8,128)S(1)}, bf16[256,256]{1,0:T(8,128)(2,1)S(1)}, bf16[64,64]{1,0:T(8,128)(2,1)S(1)}, f32[8,128]{1,0:T(8,128)S(1)}, f32[4,4,256,256]{3,2,1,0:T(8,128)S(1)}) custom-call(f32[2,2,512]{2,1,0:T(2,128)} %vis_hbm.1, s32[2,1,512]{2,1,0:T(1,128)} %bitcast.3, s32[2,512]{1,0:T(2,128)} %within_hbm.1, s32[2,512]{1,0:T(2,128)} %column_hbm.1, ...), custom_call_target="tpu_custom_call" | custom-call | tf_op jit(solution)/shard_map/gather_fields/pallas_call | solution.py:315
  12.0 5.6 %grid_visibilities.1 = (f32[4,4,256,256]{3,2,1,0:T(8,128)S(1)}, bf16[4,512,256]{2,1,0:T(8,128)(2,1)S(1)}, bf16[4,512,256]{2,1,0:T(8,128)(2,1)S(1)}) custom-call(f32[4,4,24,128]{3,2,1,0:T(8,128)S(1)} %get-tuple-element.12.f_ref, bf16[256,256]{1,0:T(8,128)(2,1)S(1)} %get-tuple-element.13.fine_ref, ...), custom_call_target="tpu_custom_call", output_to_operand_aliasing={{0}: (4, {})} | custom-call | tf_op jit(solution)/shard_map/grid_visibilities/pallas_call | solution.py:437
  17.6 20.3 %power_and_spectrum.1 = (f32[128,256]{1,0:T(8,128)S(1)}, f32[8,128]{1,0:T(8,128)S(1)}) custom-call(f32[4,4,256,256]{3,2,1,0:T(8,128)S(1)} %get-tuple-element.17.h_ref, bf16[4,512,256]{2,1,0:T(8,128)(2,1)S(1)} %get-tuple-element.18.dh_ref, bf16[4,512,256]{2,1,0:T(8,128)(2,1)S(1)} %get-tuple-element.19.dl_ref, s32[256,1024]{1,0:T(8,128)} %bins_hbm.1), custom_call_target="tpu_custom_call" | custom-call | tf_op jit(solution)/shard_map/power_and_spectrum/pallas_call | solution.py:644
  37.8 0.7 %finish.1 = (f32[128,256]{1,0:T(8,128)}, f32[512]{0:T(512)}) custom-call(f32[128,256]{1,0:T(8,128)S(1)} %get-tuple-element.20.share_ref, f32[8,128]{1,0:T(8,128)S(1)} %get-tuple-element.21.sums_ref), custom_call_target="tpu_custom_call" | custom-call | tf_op jit(solution)/shard_map/finish/pallas_call | solution.py:687
